TPU v7x, 32 devices: a whole 2x2x4 slice. The times are simulated.
32 devices in a mesh: row: 16 (over z, x, core), col: 2 (over y).
Axes of the slice: x: 2, y: 2, z: 4, core: 2. Of those that a mesh axis runs over, the one named last changes fastest.
Arguments:
- tokens: bfloat16 [1024, 8192], P('row', 'col'), may hold values from -6 to 6
- norm_gain: bfloat16 [8192], P('col'), may hold values from 0.099609375 to 1.8984375
- gate_proj: bfloat16 [8192, 28672], P('col', 'row'), may hold values from -0.0625 to 0.0625
- up_proj: bfloat16 [8192, 28672], P('col', 'row'), may hold values from -0.0625 to 0.0625
- down_proj: bfloat16 [28672, 8192], P('row', 'col'), may hold values from -0.03125 to 0.03125
Outputs:
- mixed: bfloat16 [1024, 8192], P('row', 'col')
All inputs are finite; a program needn't handle non-finite values.
Results may differ from a plain program's by a relative error of at most 0.015.
Values may be sent and summed in bfloat16 or wider, within the bound.
A program may use at most 128 MiB of HBM per device.

v0:
```python
import functools

import jax
import jax.numpy as jnp
from jax import lax
from jax.experimental import pallas as pl
from jax.experimental.pallas import tpu as pltpu
from jax.sharding import PartitionSpec as P

floor_term = 0.25
MESH = pl.DeviceIdType.MESH
BF = jnp.bfloat16
F32 = jnp.float32


def places(rows):
    n = rows // 2
    row, col = lax.axis_index("row"), lax.axis_index("col")
    core, chip = row % 2, row // 2
    z, x = chip // 2, chip % 2
    pos = z + x * (n - 1 - 2 * z)

    def at(p):
        p = (p + n) % n
        far = (2 * p) // n
        return ((1 - far) * 2 * p + far * (2 * (n - 1 - p) + 1)) * 2 + core

    right, left = (at(pos + 1), col), (at(pos - 1), col)
    return core, col, right, left, (row + 1 - 2 * core, col), (row, 1 - col)


def greet(partners):
    barrier = pltpu.get_barrier_semaphore()
    for device in partners:
        pl.semaphore_signal(barrier, inc=1, device_id=device, device_id_type=MESH)
    pl.semaphore_wait(barrier, len(partners))


def remote(src, dst, send, recv, device):
    return pltpu.make_async_remote_copy(
        src_ref=src, dst_ref=dst, send_sem=send, recv_sem=recv, device_id=device, device_id_type=MESH
    )


def first_kernel(rows, cols, tile, tok, gain, wg_hbm, wu_hbm, hid, wg, wu, x, pb, rv, sq, sq_in,
                 w_sem, sq_sem, ring_s, ring_r, sib_s, sib_r, y_s, y_r):
    n = rows // 2
    half, width = tok.shape[0] // 2, tok.shape[1]
    units = wg.shape[1]
    load_g = pltpu.make_async_copy(wg_hbm, wg, w_sem.at[0])
    load_u = pltpu.make_async_copy(wu_hbm, wu, w_sem.at[1])
    load_g.start()
    load_u.start()
    core, col, right, left, sibling, across = places(rows)
    wide = tok[...].astype(F32)
    sq[...] = jnp.broadcast_to(jnp.sum(wide * wide, axis=1, keepdims=True), sq.shape)
    greet((right, left, sibling, across))
    sums = remote(sq, sq_in, sq_sem.at[0], sq_sem.at[1], across)
    sums.start()
    sums.wait()
    total = sq[:, 0:1] + sq_in[:, 0:1]
    scale = 1.0 / jnp.sqrt(total / (width * cols) + floor_term)
    normed = (tok[...].astype(F32) * gain[...].astype(F32) * scale).astype(BF)
    x[0, 0, core] = normed[:half]
    x[0, 1, core] = normed[half:]

    def ring(s, d):
        return remote(x.at[s, d, core], x.at[s + 1, d, core], ring_s.at[s, d], ring_r.at[s, d], (right, left)[d])

    def sib(s, d):
        return remote(x.at[s, d, core], x.at[s, d, core], sib_s.at[s, d], sib_r.at[s, d], sibling)

    def swap(s, g):
        return remote(pb.at[s, g, 1 - col], rv.at[s, g], y_s.at[s, g], y_r.at[s, g], across)

    def product(s, g, w):
        @pl.loop(0, units // tile)
        def _(t):
            at = pl.ds(pl.multiple_of(t * tile, tile), tile)
            part = jnp.dot(x[s].reshape(4 * half, width), w[:, at], preferred_element_type=F32)
            pb[s, g, :, :, at] = part.astype(BF).reshape(2, 2 * half, tile)
        swap(s, g).start()

    def finish(s):
        swap(s, 0).wait_recv()
        swap(s, 1).wait_recv()

        @pl.loop(0, units // tile)
        def _(t):
            at = pl.ds(pl.multiple_of(t * tile, tile), tile)
            gate = pb[s, 0, col, :, at].astype(F32) + rv[s, 0, :, at].astype(F32)
            up = pb[s, 1, col, :, at].astype(F32) + rv[s, 1, :, at].astype(F32)
            hid[s, :, at] = (gate / (1.0 + jnp.exp(-gate)) * up).astype(BF)

    def pass_on(s):
        @pl.when(s < n - 1)
        def _():
            ring(s, 0).start()
            ring(s, 1).start()

        sib(s, 0).start()
        sib(s, 1).start()

    pass_on(0)

    @pl.loop(0, n)
    def _(s):
        sib(s, 0).wait_recv()
        sib(s, 1).wait_recv()

        @pl.when(s == 0)
        def _():
            load_g.wait()

        product(s, 0, wg)

        @pl.when(s == 0)
        def _():
            load_u.wait()

        @pl.when(s < n - 1)
        def _():
            ring(s, 0).wait_recv()
            ring(s, 1).wait_recv()
            pass_on(s + 1)

        product(s, 1, wu)

        @pl.when(s > 1)
        def _():
            finish(s - 2)

    @pl.loop(n - 2, n)
    def _(s):
        finish(s)

    @pl.loop(0, n)
    def _(s):
        for d in range(2):
            sib(s, d).wait_send()
            swap(s, d).wait_send()

        @pl.when(s < n - 1)
        def _():
            ring(s, 0).wait_send()
            ring(s, 1).wait_send()


def second_kernel(rows, tile, hid, tok, wd_hbm, out, wd, hb, pb, r1, rr, sn,
                  w_sem, h_sem, y_s, y_r, sib_s, sib_r, ring_s, ring_r):
    n = rows // 2
    half, width = tok.shape[0] // 2, tok.shape[1]
    piece = width // 2
    units = wd.shape[0]
    core, col, right, left, sibling, across = places(rows)
    load = pltpu.make_async_copy(wd_hbm, wd, w_sem)
    load.start()
    mine = pltpu.make_async_copy(hid, hb.at[col], h_sem)
    mine.start()
    rr[n - 1] = jnp.zeros(rr.shape[1:], BF)
    greet((right, left, sibling, across))

    def swap(s):
        return remote(hid.at[s], hb.at[col, s], y_s.at[s], y_r.at[s], across)

    def sib(s, d, k):
        return remote(pb.at[s, d, 1 - core, k], r1.at[s, d, k], sib_s.at[s, d, k], sib_r.at[s, d, k], sibling)

    def ring(s, d, k):
        return remote(sn.at[s, d, k], rr.at[s - 1, d, k], ring_s.at[s, d, k], ring_r.at[s, d, k], (left, right)[d])

    @pl.loop(0, n)
    def _(i):
        swap(n - 1 - i).start()

    mine.wait()
    load.wait()

    def product(s, k):
        @pl.loop(0, piece // tile)
        def _(t):
            start = pl.multiple_of(t * tile, tile)
            w = wd[:, pl.ds(pl.multiple_of(k * piece + t * tile, tile), tile)]
            h = jnp.concatenate([hb[0, s], hb[1, s]], axis=0)
            part = jnp.dot(h, w, preferred_element_type=F32).astype(BF)
            pb[s, :, :, k, :, pl.ds(start, tile)] = part.reshape(2, 2, half, tile)
        sib(s, 0, k).start()
        sib(s, 1, k).start()

    def added(s, d, k):
        return pb[s, d, core, k].astype(F32) + r1[s, d, k].astype(F32) + rr[s, d, k].astype(F32)

    def stage(s, k):
        for d in range(2):
            sib(s, d, k).wait_recv()

            @pl.when(s < n - 1)
            def _():
                ring(s + 1, d, k).wait_recv()

            sn[s, d, k] = added(s, d, k).astype(BF)
            ring(s, d, k).start()

    @pl.loop(0, n)
    def _(i):
        s = n - 1 - i
        swap(s).wait_recv()
        product(s, 0)

        @pl.when(i > 0)
        def _():
            stage(s + 1, 1)

        product(s, 1)

        @pl.when(s > 0)
        def _():
            stage(s, 0)

    for k in range(2):
        for d in range(2):
            sib(0, d, k).wait_recv()
            ring(1, d, k).wait_recv()
            here = (slice(d * half, (d + 1) * half), slice(k * piece, (k + 1) * piece))
            out[here] = (tok[here].astype(F32) + added(0, d, k)).astype(BF)

    @pl.loop(0, n)
    def _(s):
        swap(s).wait_send()
        for d in range(2):
            for k in range(2):
                sib(s, d, k).wait_send()

        @pl.when(s > 0)
        def _():
            for d in range(2):
                for k in range(2):
                    ring(s, d, k).wait_send()


def kernels(rows, cols, tokens, norm_gain, gate_proj, up_proj, down_proj):
    n = rows // 2
    count, width = tokens.shape
    half = count // 2
    units = gate_proj.shape[1]
    tile = 256 if units % 256 == 0 else 128
    vmem, hbm = pl.BlockSpec(memory_space=pltpu.VMEM), pl.BlockSpec(memory_space=pl.ANY)
    dma = pltpu.SemaphoreType.DMA
    hidden = pl.pallas_call(
        functools.partial(first_kernel, rows, cols, tile),
        out_shape=jax.ShapeDtypeStruct((n, 2 * half, units), BF),
        in_specs=[vmem, vmem, hbm, hbm],
        out_specs=vmem,
        scratch_shapes=[
            pltpu.VMEM(gate_proj.shape, BF),
            pltpu.VMEM(up_proj.shape, BF),
            pltpu.VMEM((n, 2, 2, half, width), BF),
            pltpu.VMEM((n, 2, 2, 2 * half, units), BF),
            pltpu.VMEM((n, 2, 2 * half, units), BF),
            pltpu.VMEM((count, 128), F32),
            pltpu.VMEM((count, 128), F32),
            dma((2,)), dma((2,)),
            dma((n, 2)), dma((n, 2)), dma((n, 2)), dma((n, 2)), dma((n, 2)), dma((n, 2)),
        ],
        compiler_params=pltpu.CompilerParams(
            collective_id=0, has_side_effects=True, vmem_limit_bytes=60 * 1024 * 1024
        ),
    )(tokens, norm_gain.reshape(1, width), gate_proj, up_proj)
    return pl.pallas_call(
        functools.partial(second_kernel, rows, 256),
        out_shape=jax.ShapeDtypeStruct(tokens.shape, BF),
        in_specs=[hbm, vmem, hbm],
        out_specs=vmem,
        scratch_shapes=[
            pltpu.VMEM(down_proj.shape, BF),
            pltpu.VMEM((2, n, 2 * half, units), BF),
            pltpu.VMEM((n, 2, 2, 2, half, width // 2), BF),
            pltpu.VMEM((n, 2, 2, half, width // 2), BF),
            pltpu.VMEM((n, 2, 2, half, width // 2), BF),
            pltpu.VMEM((n, 2, 2, half, width // 2), BF),
            dma, dma,
            dma((n,)), dma((n,)), dma((n, 2, 2)), dma((n, 2, 2)), dma((n, 2, 2)), dma((n, 2, 2)),
        ],
        compiler_params=pltpu.CompilerParams(
            collective_id=1, has_side_effects=True, vmem_limit_bytes=60 * 1024 * 1024
        ),
    )(hidden, tokens, down_proj)


def plain(rows, cols, tokens, norm_gain, gate_proj, up_proj, down_proj):
    gathered = lax.all_gather(tokens, "row", axis=0, tiled=True)
    widened = gathered.astype(jnp.float32)
    partial_squares = jnp.sum(widened * widened, axis=1)
    scaled = (widened * norm_gain.astype(jnp.float32)[None, :]).astype(jnp.bfloat16)
    gate_part = jnp.dot(scaled, gate_proj, preferred_element_type=jnp.float32)
    up_part = jnp.dot(scaled, up_proj, preferred_element_type=jnp.float32)
    gate_sum, up_sum, block_squares = (
        lax.psum_scatter(
            gate_part.astype(jnp.bfloat16), "col", scatter_dimension=0, tiled=True
        ).astype(jnp.float32),
        lax.psum_scatter(
            up_part.astype(jnp.bfloat16), "col", scatter_dimension=0, tiled=True
        ).astype(jnp.float32),
        lax.psum_scatter(
            partial_squares.astype(jnp.bfloat16), "col", scatter_dimension=0, tiled=True
        ).astype(jnp.float32),
    )
    row_scale = 1.0 / jnp.sqrt(block_squares / (tokens.shape[1] * cols) + floor_term)
    gate_value = row_scale[:, None] * gate_sum
    up_value = row_scale[:, None] * up_sum
    hidden = (jax.nn.silu(gate_value) * up_value).astype(jnp.bfloat16)
    partial_out = jnp.dot(
        lax.all_gather(hidden, "col", axis=0, tiled=True),
        down_proj,
        preferred_element_type=jnp.float32,
    )
    summed = lax.psum_scatter(
        partial_out.astype(jnp.bfloat16), "row", scatter_dimension=0, tiled=True
    ).astype(jnp.float32)
    return (tokens.astype(jnp.float32) + summed).astype(jnp.bfloat16)


def solution(mesh):
    rows, cols = mesh.shape["row"], mesh.shape["col"]
    body = kernels if cols == 2 and rows % 4 == 0 and rows >= 8 else plain
    in_specs = (P("row", "col"), P("col"), P("col", "row"), P("col", "row"), P("row", "col"))
    out_specs = P("row", "col")
    return jax.shard_map(
        functools.partial(body, rows, cols), mesh=mesh, in_specs=in_specs, out_specs=out_specs, check_vma=False
    )
```

profile of v0, /device:TPU:0, one launch (start us, length us, event | category | flops | bytes accessed | tf_op | source)
XLA Modules:
  0.0 157.1 jit_solution(11033407475791327460)
XLA Ops:
  0.0 1.3 reshape.3.gain
  1.3 95.4 %shard_map.55.hid = bf16[8,64,1792]{2,1,0:T(8,128)(2,1)} custom-call(bf16[64,4096]{1,0:T(8,128)(2,1)} %tok.3, bf16[1,4096]{1,0:T(2,128)(2,1)} %reshape.3.gain, bf16[4096,1792]{1,0:T(8,128)(2,1)} %wg_hbm.1, bf16[4096,1792]{1,0:T(8,128)(2,1)} %wu_hbm.1), custom_call_target="tpu_custom_call" | custom-call | tf_op jit(solution)/shard_map/pallas_call | solution.py:249
  96.7 58.5 %shard_map.56 = bf16[64,4096]{1,0:T(8,128)(2,1)} custom-call(bf16[8,64,1792]{2,1,0:T(8,128)(2,1)} %shard_map.55.hid, bf16[64,4096]{1,0:T(8,128)(2,1)} %tok.3, bf16[1792,4096]{1,0:T(8,128)(2,1)} %wd_hbm.1), custom_call_target="tpu_custom_call" | custom-call | tf_op jit(solution)/shard_map/pallas_call | solution.py:269
  155.2 1.9 %copy.7 = bf16[64,4096]{1,0:T(8,128)(2,1)} copy(bf16[64,4096]{1,0:T(8,128)(2,1)} %shard_map.56) | data formatting | bytes 1048576
where the time goes:
time: 157 us
  Pallas kernels  154 us (98%)
  local copies, waits for them, and re-layouts  3.18 us (2%)
    pallas_call x1, Pallas kernels, kernels(): pl.pallas_call(functools.partial(first_kernel, rows, cols, tile), out_sha...  95.4 us
    pallas_call x1, Pallas kernels, kernels(): pl.pallas_call(functools.partial(second_kernel, rows, 256), out_shape=jax...  58.5 us

commit v1 on v0

v1 whole, which is shorter than its diff:
```python
import functools

import jax
import jax.numpy as jnp
from jax import lax
from jax.experimental import pallas as pl
from jax.experimental.pallas import tpu as pltpu
from jax.sharding import PartitionSpec as P

floor_term = 0.25
MESH = pl.DeviceIdType.MESH
BF = jnp.bfloat16
F32 = jnp.float32


def places(rows):
    n = rows // 2
    row, col = lax.axis_index("row"), lax.axis_index("col")
    core, chip = row % 2, row // 2
    z, x = chip // 2, chip % 2
    pos = z + x * (n - 1 - 2 * z)

    def at(p):
        p = (p + n) % n
        far = (2 * p) // n
        return ((1 - far) * 2 * p + far * (2 * (n - 1 - p) + 1)) * 2 + core

    right, left = (at(pos + 1), col), (at(pos - 1), col)
    return core, col, right, left, (row + 1 - 2 * core, col), (row, 1 - col)


def greet(partners):
    barrier = pltpu.get_barrier_semaphore()
    for device in partners:
        pl.semaphore_signal(barrier, inc=1, device_id=device, device_id_type=MESH)
    return lambda: pl.semaphore_wait(barrier, len(partners))


def remote(src, dst, send, recv, device):
    return pltpu.make_async_remote_copy(
        src_ref=src, dst_ref=dst, send_sem=send, recv_sem=recv, device_id=device, device_id_type=MESH
    )


def fused_kernel(rows, cols, tile, lead, tok_hbm, gain, wg_hbm, wu_hbm, wd_hbm, out, wg, wu, wd, x, pb, rv, pd, kept, sq, sq_in, sc,
                 tok_sem, wg_sem, wu_sem, wd_sem, sq_sem, ring_s, ring_r, sib_s, sib_r, lead_s, lead_r, y_s, y_r,
                 ds_s, ds_r, rs_s, rs_r, sc_s, sc_r, free):
    n = rows // 2
    half, width = out.shape[0] // 2, out.shape[1]
    units = wg.shape[1]
    leads = units // lead
    keep = pb.shape[0]
    parts, piece = pd.shape[1], pd.shape[5]
    core, col, right, left, sibling, across = places(rows)
    load_tok = pltpu.make_async_copy(tok_hbm, out, tok_sem)
    load_d = pltpu.make_async_copy(wd_hbm, wd, wd_sem)

    def lead_cols(t):
        return pl.ds(pl.multiple_of(t * lead, lead), lead)

    def load_g(t):
        return pltpu.make_async_copy(wg_hbm.at[:, lead_cols(t)], wg.at[:, lead_cols(t)], wg_sem.at[t])

    def load_u(t):
        return pltpu.make_async_copy(wu_hbm.at[:, lead_cols(t)], wu.at[:, lead_cols(t)], wu_sem.at[t])

    def scale_ring(s):
        onward = (jnp.where(col == 0, right[0], left[0]), col)
        return remote(sc.at[s, core], sc.at[s + 1, core], sc_s.at[s, 0], sc_r.at[s, 0], onward)

    def scale_sib(s):
        return remote(sc.at[s, core], sc.at[s, core], sc_s.at[s, 1], sc_r.at[s, 1], sibling)

    def scale_on(s):
        scale_sib(s).start()

        @pl.when(s < n - 1)
        def _():
            scale_ring(s).start()

    def ring(s, d):
        return remote(x.at[s, d, core], x.at[s + 1, d, core], ring_s.at[s, d], ring_r.at[s, d], (right, left)[d])

    def sib(s, d):
        return remote(x.at[s, d, core], x.at[s, d, core], sib_s.at[s, d], sib_r.at[s, d], sibling)

    def lead_swap(g, t):
        at = lead_cols(t)
        return remote(pb.at[0, g, 1 - col, :, at], rv.at[0, g, :, at], lead_s.at[g, t], lead_r.at[g, t], across)

    def lead_sent(g):
        @pl.loop(0, leads)
        def _(t):
            lead_swap(g, t).wait_send()

    def swap(s, g):
        return remote(pb.at[s % keep, g, 1 - col], rv.at[s, g], y_s.at[s, g], y_r.at[s, g], across)

    def slot(s):
        return jnp.where(s == n - 1, 1, jnp.maximum(s - 1, 0))

    def share(s):
        return remote(rv.at[slot(s), col], rv.at[slot(s), col], y_s.at[s, 2], y_r.at[s, 2], across)

    def part_cols(k):
        return pl.ds(pl.multiple_of(k * piece, piece), piece)

    def down_sib(s, k):
        return remote(pd.at[s % 2, k, :, 1 - core], x.at[s, :, 1, :, part_cols(k)], ds_s.at[s, k], ds_r.at[s, k], sibling)

    def down_ring(s, d, k):
        return remote(pd.at[s % 2, k, d, core], x.at[(s + 1) % n, d, 0, :, part_cols(k)],
                      rs_s.at[s, d, k], rs_r.at[s, d, k], (right, left)[d])

    def product(s, g, w):
        with jax.named_scope("product"):
            @pl.loop(0, units // tile)
            def _(t):
                at = pl.ds(pl.multiple_of(t * tile, tile), tile)
                part = jnp.dot(x[s].reshape(4 * half, width), w[:, at], preferred_element_type=F32)
                pb[s % keep, g, :, :, at] = part.astype(BF).reshape(2, 2 * half, tile)
            swap(s, g).start()

    def activate(s):
        with jax.named_scope("activate"):
            scale_sib(s).wait_recv()
            scale = sc[s].reshape(2 * half, 128)[:, 0:1]

            @pl.loop(0, leads)
            def _(t):
                at = lead_cols(t)
                gate = scale * (pb[s % keep, 0, col, :, at].astype(F32) + rv[s, 0, :, at].astype(F32))
                up = scale * (pb[s % keep, 1, col, :, at].astype(F32) + rv[s, 1, :, at].astype(F32))
                hidden = (gate / (1.0 + jnp.exp(-gate)) * up).astype(BF)
                if isinstance(s, int) and s == 0:
                    kept[:, at] = hidden
                else:
                    rv[slot(s), col, :, at] = hidden

    def finish(s):
        swap(s, 0).wait_recv()
        swap(s, 1).wait_recv()
        activate(s)
        share(s).start()

    def pass_on(s):
        with jax.named_scope("pass_on"):
            sib(s, 0).start()
            sib(s, 1).start()

            @pl.when(s < n - 1)
            def _():
                ring(s, 0).start()
                ring(s, 1).start()

    def retire(s):
        with jax.named_scope("retire"):
            for d in range(2):
                sib(s, d).wait_send()

            @pl.when(s < n - 1)
            def _():
                ring(s, 0).wait_send()
                ring(s, 1).wait_send()

            pl.semaphore_signal(free.at[s, 2], inc=1, device_id=sibling, device_id_type=MESH)

            @pl.when(s != 1)
            def _():
                pl.semaphore_signal(free.at[s, 0], inc=1, device_id=left, device_id_type=MESH)
                pl.semaphore_signal(free.at[s, 1], inc=1, device_id=right, device_id_type=MESH)

    def sent(s):
        with jax.named_scope("sent"):
            @pl.loop(0, parts)
            def _(k):
                down_sib(s, k).wait_send()
                down_ring(s, 0, k).wait_send()
                down_ring(s, 1, k).wait_send()

    def down_part(s, k):
        h = rv[slot(s)].reshape(4 * half, units)
        part = jnp.dot(h, wd[:, part_cols(k)], preferred_element_type=F32).astype(BF)
        pd[s % 2, k] = part.reshape(2, 2, half, piece)
        down_sib(s, k).start()

    def stage_part(s, k):
        down_sib(s, k).wait_recv()
        for d in range(2):
            mine = pd[s % 2, k, d, core].astype(F32) + x[s, d, 1, :, part_cols(k)].astype(F32)

            @pl.when(s == 1)
            def _():
                pd[s % 2, k, d, core] = mine.astype(BF)

            @pl.when(s > 1)
            def _():
                down_ring(s - 1, d, k).wait_recv()
                pd[s % 2, k, d, core] = (mine + x[s, d, 0, :, part_cols(k)].astype(F32)).astype(BF)

            down_ring(s, d, k).start()

    def final_part(k):
        down_sib(0, k).wait_recv()
        for d in range(2):
            down_ring(n - 1, d, k).wait_recv()
            here = (slice(d * half, (d + 1) * half), part_cols(k))
            mine = pd[0, k, d, core].astype(F32) + x[0, d, 1, :, here[1]].astype(F32)
            mine = mine + x[0, d, 0, :, here[1]].astype(F32)
            out[here] = (out[here].astype(F32) + mine).astype(BF)

    def ring_free(s):
        pl.semaphore_wait(free.at[(s + 1) % n, 0], 1)
        pl.semaphore_wait(free.at[(s + 1) % n, 1], 1)

    def down(s):
        pl.semaphore_wait(free.at[s, 2], 1)
        with jax.named_scope("down"):
            @pl.loop(0, parts)
            def _(k):
                down_part(s, k)

    def stage(s):
        ring_free(s)
        with jax.named_scope("stage"):
            @pl.loop(0, parts)
            def _(k):
                stage_part(s, k)

    def last(s, follow):
        with jax.named_scope("last"):
            pl.semaphore_wait(free.at[s, 2], 1)

            @pl.loop(0, parts + 2)
            def _(k):
                @pl.when(k < parts)
                def _():
                    down_part(s, k)

                @pl.when(k > 1)
                def _():
                    follow(k - 2)

    met = greet((right, left, sibling, across))
    load_tok.start()

    @pl.loop(0, leads)
    def _(t):
        load_g(t).start()

    with jax.named_scope("tok"):
        load_tok.wait()
    gains = gain[...].astype(F32)
    squares = jnp.zeros((2 * half, 128), F32)
    for b in range(width // 128):
        at = slice(b * 128, (b + 1) * 128)
        wide = out[:, at].astype(F32)
        squares += wide * wide
        scaled = (wide * gains[b : b + 1]).astype(BF)
        x[0, 0, core, :, at] = scaled[:half]
        x[0, 1, core, :, at] = scaled[half:]
    sums = jnp.broadcast_to(jnp.sum(squares, axis=1, keepdims=True), squares.shape)
    sq[0] = sums[:half]
    sq[1] = sums[half:]
    with jax.named_scope("met"):
        met()
    pass_on(0)
    trade = remote(sq.at[1 - col], sq_in, sq_sem.at[0], sq_sem.at[1], across)
    trade.start()
    with jax.named_scope("sib0"):
        sib(0, 0).wait_recv()
        sib(0, 1).wait_recv()

    def lead_product(g, w, load):
        @pl.loop(0, leads)
        def _(t):
            load(t).wait()
            at = lead_cols(t)
            part = jnp.dot(x[0].reshape(4 * half, width), w[:, at], preferred_element_type=F32)
            pb[0, g, :, :, at] = part.astype(BF).reshape(2, 2 * half, lead)
            lead_swap(g, t).start()

            if g == 0:
                load_u(t).start()

    with jax.named_scope("lead0"):
        lead_product(0, wg, load_g)
    load_d.start()
    trade.wait()
    total = sq[col] + sq_in[...]
    sc[0, core] = 1.0 / jnp.sqrt(total / (width * cols) + floor_term)
    scale_on(0)
    with jax.named_scope("lead1"):
        lead_product(1, wu, load_u)
    with jax.named_scope("ring0"):
        ring(0, 0).wait_recv()
        ring(0, 1).wait_recv()
    pass_on(1)
    scale_ring(0).wait_recv()
    scale_on(1)

    @pl.loop(1, n)
    def _(i):
        sib(i, 0).wait_recv()
        sib(i, 1).wait_recv()

        @pl.when(i == keep)
        def _():
            lead_sent(0)

        @pl.when(i > keep)
        def _():
            swap(i - keep, 0).wait_send()

        product(i, 0, wg)

        @pl.when(i == 1)
        def _():
            @pl.loop(0, leads)
            def _(t):
                lead_swap(0, t).wait_recv()
                lead_swap(1, t).wait_recv()

            activate(0)

        @pl.when((i > 1) & (i < n - 1))
        def _():
            finish(i - 1)

        @pl.when(i == keep)
        def _():
            lead_sent(1)

        @pl.when(i > keep)
        def _():
            swap(i - keep, 1).wait_send()

        product(i, 1, wu)

        @pl.when(i < n - 1)
        def _():
            ring(i, 0).wait_recv()
            ring(i, 1).wait_recv()
            pass_on(i + 1)
            scale_ring(i).wait_recv()
            scale_on(i + 1)

        retire(i - 1)

        @pl.when(i > 3)
        def _():
            stage(i - 3)

        @pl.when(i == n - 1)
        def _():
            finish(i - 1)

        @pl.when(i == 3)
        def _():
            load_d.wait()

        @pl.when(i > 2)
        def _():
            share(i - 2).wait_recv()

            @pl.when(i > 4)
            def _():
                sent(i - 4)

            down(i - 2)

    retire(n - 1)
    stage(n - 3)
    share(1).wait_send()
    share(2).wait_send()
    rv[0, col] = kept[...]
    finish(n - 1)
    share(0).start()
    sent(n - 4)
    ring_free(n - 2)
    with jax.named_scope("share6"):
        share(n - 2).wait_recv()
    last(n - 2, lambda k: stage_part(n - 2, k))
    sent(n - 3)
    ring_free(n - 1)
    with jax.named_scope("share7"):
        share(n - 1).wait_recv()
    last(n - 1, lambda k: stage_part(n - 1, k))
    sent(n - 2)
    with jax.named_scope("share0"):
        share(0).wait_recv()
    last(0, final_part)

    sent(n - 1)

    @pl.loop(0, parts)
    def _(k):
        down_sib(0, k).wait_send()

    @pl.loop(n - keep, n)
    def _(s):
        swap(s, 0).wait_send()
        swap(s, 1).wait_send()

    @pl.loop(0, n)
    def _(s):
        @pl.when((s < 1) | (s > 2))
        def _():
            share(s).wait_send()

        scale_sib(s).wait_send()

        @pl.when(s < n - 1)
        def _():
            scale_ring(s).wait_send()


def kernels(rows, cols, tokens, norm_gain, gate_proj, up_proj, down_proj):
    n = rows // 2
    count, width = tokens.shape
    half = count // 2
    units = gate_proj.shape[1]
    lead = 256 if units % 256 == 0 else 128
    tile = units // 2 if units % 256 == 0 else lead
    parts = 4
    piece = width // parts
    vmem, hbm = pl.BlockSpec(memory_space=pltpu.VMEM), pl.BlockSpec(memory_space=pl.ANY)
    dma = pltpu.SemaphoreType.DMA
    return pl.pallas_call(
        functools.partial(fused_kernel, rows, cols, tile, lead),
        out_shape=jax.ShapeDtypeStruct(tokens.shape, BF),
        in_specs=[hbm, vmem, hbm, hbm, hbm],
        out_specs=vmem,
        scratch_shapes=[
            pltpu.VMEM(gate_proj.shape, BF),
            pltpu.VMEM(up_proj.shape, BF),
            pltpu.VMEM(down_proj.shape, BF),
            pltpu.VMEM((n, 2, 2, half, width), BF),
            pltpu.VMEM((4, 2, 2, 2 * half, units), BF),
            pltpu.VMEM((n, 2, 2 * half, units), BF),
            pltpu.VMEM((2, parts, 2, 2, half, piece), BF),
            pltpu.VMEM((2 * half, units), BF),
            pltpu.VMEM((2, half, 128), F32),
            pltpu.VMEM((half, 128), F32),
            pltpu.VMEM((n, 2, half, 128), F32),
            dma, dma((units // lead,)), dma((units // lead,)), dma, dma((2,)),
            dma((n, 2)), dma((n, 2)), dma((n, 2)), dma((n, 2)),
            dma((2, units // lead)), dma((2, units // lead)),
            dma((n, 3)), dma((n, 3)),
            dma((n, parts)), dma((n, parts)), dma((n, 2, parts)), dma((n, 2, parts)),
            dma((n, 2)), dma((n, 2)),
            pltpu.SemaphoreType.REGULAR((n, 3)),
        ],
        compiler_params=pltpu.CompilerParams(
            collective_id=0, has_side_effects=True, vmem_limit_bytes=67043328
        ),
    )(tokens, norm_gain.reshape(width // 128, 128), gate_proj, up_proj, down_proj)


def plain(rows, cols, tokens, norm_gain, gate_proj, up_proj, down_proj):
    gathered = lax.all_gather(tokens, "row", axis=0, tiled=True)
    widened = gathered.astype(jnp.float32)
    partial_squares = jnp.sum(widened * widened, axis=1)
    scaled = (widened * norm_gain.astype(jnp.float32)[None, :]).astype(jnp.bfloat16)
    gate_part = jnp.dot(scaled, gate_proj, preferred_element_type=jnp.float32)
    up_part = jnp.dot(scaled, up_proj, preferred_element_type=jnp.float32)
    gate_sum, up_sum, block_squares = (
        lax.psum_scatter(
            gate_part.astype(jnp.bfloat16), "col", scatter_dimension=0, tiled=True
        ).astype(jnp.float32),
        lax.psum_scatter(
            up_part.astype(jnp.bfloat16), "col", scatter_dimension=0, tiled=True
        ).astype(jnp.float32),
        lax.psum_scatter(
            partial_squares.astype(jnp.bfloat16), "col", scatter_dimension=0, tiled=True
        ).astype(jnp.float32),
    )
    row_scale = 1.0 / jnp.sqrt(block_squares / (tokens.shape[1] * cols) + floor_term)
    gate_value = row_scale[:, None] * gate_sum
    up_value = row_scale[:, None] * up_sum
    hidden = (jax.nn.silu(gate_value) * up_value).astype(jnp.bfloat16)
    partial_out = jnp.dot(
        lax.all_gather(hidden, "col", axis=0, tiled=True),
        down_proj,
        preferred_element_type=jnp.float32,
    )
    summed = lax.psum_scatter(
        partial_out.astype(jnp.bfloat16), "row", scatter_dimension=0, tiled=True
    ).astype(jnp.float32)
    return (tokens.astype(jnp.float32) + summed).astype(jnp.bfloat16)


def solution(mesh):
    rows, cols = mesh.shape["row"], mesh.shape["col"]
    body = kernels if cols == 2 and rows % 4 == 0 and rows >= 16 else plain
    in_specs = (P("row", "col"), P("col"), P("col", "row"), P("col", "row"), P("row", "col"))
    out_specs = P("row", "col")
    return jax.shard_map(
        functools.partial(body, rows, cols), mesh=mesh, in_specs=in_specs, out_specs=out_specs, check_vma=False
    )
```

time: 157 us -> 140 us (0.89)
  Pallas kernels: 154 us -> 138 us
    pallas_call x2 -> x1, Pallas kernels: 154 us -> 138 us  [kernels(): pl.pallas_call(functools.partial(fused_kernel, rows, cols, tile, lead), o...]
where the time goes in v1:
time: 140 us
  Pallas kernels  138 us (99%)
  local copies, waits for them, and re-layouts  1.87 us (1%)
    pallas_call x1, Pallas kernels, kernels(): pl.pallas_call(functools.partial(fused_kernel, rows, cols, tile, lead), o...  138 us

profile of v1, /device:TPU:0, one launch (start us, length us, event | category | flops | bytes accessed | tf_op | source)
XLA Modules:
  0.0 140.1 jit_solution(16271944195335200548)
XLA Ops:
  0.0 138.3 %shard_map.55 = bf16[64,4096]{1,0:T(8,128)(2,1)} custom-call(bf16[64,4096]{1,0:T(8,128)(2,1)} %tok_hbm.1, bf16[32,128]{1,0:T(8,128)(2,1)} %bitcast.1, bf16[4096,1792]{1,0:T(8,128)(2,1)} %wg_hbm.1, bf16[4096,1792]{1,0:T(8,128)(2,1)} %wu_hbm.1, bf16[1792,4096]{1,0:T(8,128)(2,1)} %wd_hbm.1), custom_call_target="tpu_custom_call" | custom-call | tf_op jit(solution)/shard_map/pallas_call | solution.py:429
  138.3 1.9 %copy.7 = bf16[64,4096]{1,0:T(8,128)(2,1)} copy(bf16[64,4096]{1,0:T(8,128)(2,1)} %shard_map.55) | data formatting | bytes 1048576

commit v2 on v1

--- a/solution.py
+++ b/solution.py
@@ -43,7 +43,7 @@
 
 
 def fused_kernel(rows, cols, tile, lead, tok_hbm, gain, wg_hbm, wu_hbm, wd_hbm, out, wg, wu, wd, x, pb, rv, pd, kept, sq, sq_in, sc,
-                 tok_sem, wg_sem, wu_sem, wd_sem, sq_sem, ring_s, ring_r, sib_s, sib_r, lead_s, lead_r, y_s, y_r,
+                 tok_sem, w_sem, wd_sem, sq_sem, ring_s, ring_r, sib_s, sib_r, y_s, y_r,
                  ds_s, ds_r, rs_s, rs_r, sc_s, sc_r, free):
     n = rows // 2
     half, width = out.shape[0] // 2, out.shape[1]
@@ -59,19 +59,24 @@
         return pl.ds(pl.multiple_of(t * lead, lead), lead)
 
     def load_g(t):
-        return pltpu.make_async_copy(wg_hbm.at[:, lead_cols(t)], wg.at[:, lead_cols(t)], wg_sem.at[t])
+        return pltpu.make_async_copy(wg_hbm.at[:, lead_cols(t)], wg.at[:, lead_cols(t)], w_sem.at[t])
 
     def load_u(t):
-        return pltpu.make_async_copy(wu_hbm.at[:, lead_cols(t)], wu.at[:, lead_cols(t)], wu_sem.at[t])
+        return pltpu.make_async_copy(wu_hbm.at[:, lead_cols(t)], wu.at[:, lead_cols(t)], w_sem.at[t])
 
     def scale_ring(s):
         onward = (jnp.where(col == 0, right[0], left[0]), col)
-        return remote(sc.at[s, core], sc.at[s + 1, core], sc_s.at[s, 0], sc_r.at[s, 0], onward)
+        return remote(sc.at[s, core], sc.at[s + 1, core], sc_s.at[s % 2, 0], sc_r.at[s, 0], onward)
 
     def scale_sib(s):
-        return remote(sc.at[s, core], sc.at[s, core], sc_s.at[s, 1], sc_r.at[s, 1], sibling)
+        return remote(sc.at[s, core], sc.at[s, core], sc_s.at[s % 2, 1], sc_r.at[s, 1], sibling)
 
     def scale_on(s):
+        @pl.when(s > 1)
+        def _():
+            scale_sib(s - 2).wait_send()
+            scale_ring(s - 2).wait_send()
+
         scale_sib(s).start()
 
         @pl.when(s < n - 1)
@@ -79,38 +84,29 @@
             scale_ring(s).start()
 
     def ring(s, d):
-        return remote(x.at[s, d, core], x.at[s + 1, d, core], ring_s.at[s, d], ring_r.at[s, d], (right, left)[d])
-
-    def sib(s, d):
-        return remote(x.at[s, d, core], x.at[s, d, core], sib_s.at[s, d], sib_r.at[s, d], sibling)
-
-    def lead_swap(g, t):
-        at = lead_cols(t)
-        return remote(pb.at[0, g, 1 - col, :, at], rv.at[0, g, :, at], lead_s.at[g, t], lead_r.at[g, t], across)
-
-    def lead_sent(g):
-        @pl.loop(0, leads)
-        def _(t):
-            lead_swap(g, t).wait_send()
-
-    def swap(s, g):
-        return remote(pb.at[s % keep, g, 1 - col], rv.at[s, g], y_s.at[s, g], y_r.at[s, g], across)
+        return remote(x.at[s, d, core], x.at[s + 1, d, core], ring_s.at[s % 2, d], ring_r.at[s, d], (right, left)[d])
+
+    def sib(s):
+        return remote(x.at[s, :, core], x.at[s, :, core], sib_s.at[s % 2], sib_r.at[s], sibling)
+
+    def swap(s, g, at=slice(None)):
+        return remote(pb.at[s % keep, g, 1 - col, :, at], rv.at[s, g, :, at], y_s.at[s % keep, g], y_r.at[s % keep, g], across)
 
     def slot(s):
         return jnp.where(s == n - 1, 1, jnp.maximum(s - 1, 0))
 
     def share(s):
-        return remote(rv.at[slot(s), col], rv.at[slot(s), col], y_s.at[s, 2], y_r.at[s, 2], across)
+        return remote(rv.at[slot(s), col], rv.at[slot(s), col], y_s.at[s % keep, 2], y_r.at[s % keep, 2], across)
 
     def part_cols(k):
         return pl.ds(pl.multiple_of(k * piece, piece), piece)
 
     def down_sib(s, k):
-        return remote(pd.at[s % 2, k, :, 1 - core], x.at[s, :, 1, :, part_cols(k)], ds_s.at[s, k], ds_r.at[s, k], sibling)
+        return remote(pd.at[s % 2, k, :, 1 - core], x.at[s, :, 1, :, part_cols(k)], ds_s.at[s % 2, k], ds_r.at[jnp.where(s == 0, 2, s % 2), k], sibling)
 
     def down_ring(s, d, k):
         return remote(pd.at[s % 2, k, d, core], x.at[(s + 1) % n, d, 0, :, part_cols(k)],
-                      rs_s.at[s, d, k], rs_r.at[s, d, k], (right, left)[d])
+                      rs_s.at[s % 2, d, k], rs_r.at[jnp.where(s == n - 1, 2, s % 2), d, k], (right, left)[d])
 
     def product(s, g, w):
         with jax.named_scope("product"):
@@ -119,7 +115,7 @@
                 at = pl.ds(pl.multiple_of(t * tile, tile), tile)
                 part = jnp.dot(x[s].reshape(4 * half, width), w[:, at], preferred_element_type=F32)
                 pb[s % keep, g, :, :, at] = part.astype(BF).reshape(2, 2 * half, tile)
-            swap(s, g).start()
+                swap(s, g, at).start()
 
     def activate(s):
         with jax.named_scope("activate"):
@@ -141,12 +137,16 @@
         swap(s, 0).wait_recv()
         swap(s, 1).wait_recv()
         activate(s)
+
+        @pl.when(s > keep)
+        def _():
+            share(s - keep).wait_send()
+
         share(s).start()
 
     def pass_on(s):
         with jax.named_scope("pass_on"):
-            sib(s, 0).start()
-            sib(s, 1).start()
+            sib(s).start()
 
             @pl.when(s < n - 1)
             def _():
@@ -155,8 +155,7 @@
 
     def retire(s):
         with jax.named_scope("retire"):
-            for d in range(2):
-                sib(s, d).wait_send()
+            sib(s).wait_send()
 
             @pl.when(s < n - 1)
             def _():
@@ -268,8 +267,7 @@
     trade = remote(sq.at[1 - col], sq_in, sq_sem.at[0], sq_sem.at[1], across)
     trade.start()
     with jax.named_scope("sib0"):
-        sib(0, 0).wait_recv()
-        sib(0, 1).wait_recv()
+        sib(0).wait_recv()
 
     def lead_product(g, w, load):
         @pl.loop(0, leads)
@@ -278,10 +276,19 @@
             at = lead_cols(t)
             part = jnp.dot(x[0].reshape(4 * half, width), w[:, at], preferred_element_type=F32)
             pb[0, g, :, :, at] = part.astype(BF).reshape(2, 2 * half, lead)
-            lead_swap(g, t).start()
+            swap(0, g, at).start()
 
             if g == 0:
                 load_u(t).start()
+            else:
+
+                @pl.when(t == leads - 2)
+                def _():
+                    ring(0, 0).wait_recv()
+                    ring(0, 1).wait_recv()
+                    pass_on(1)
+                    scale_ring(0).wait_recv()
+                    scale_on(1)
 
     with jax.named_scope("lead0"):
         lead_product(0, wg, load_g)
@@ -292,23 +299,12 @@
     scale_on(0)
     with jax.named_scope("lead1"):
         lead_product(1, wu, load_u)
-    with jax.named_scope("ring0"):
-        ring(0, 0).wait_recv()
-        ring(0, 1).wait_recv()
-    pass_on(1)
-    scale_ring(0).wait_recv()
-    scale_on(1)
 
     @pl.loop(1, n)
     def _(i):
-        sib(i, 0).wait_recv()
-        sib(i, 1).wait_recv()
-
-        @pl.when(i == keep)
-        def _():
-            lead_sent(0)
-
-        @pl.when(i > keep)
+        sib(i).wait_recv()
+
+        @pl.when(i >= keep)
         def _():
             swap(i - keep, 0).wait_send()
 
@@ -316,26 +312,25 @@
 
         @pl.when(i == 1)
         def _():
-            @pl.loop(0, leads)
-            def _(t):
-                lead_swap(0, t).wait_recv()
-                lead_swap(1, t).wait_recv()
-
+            swap(0, 0).wait_recv()
+            swap(0, 1).wait_recv()
             activate(0)
 
         @pl.when((i > 1) & (i < n - 1))
         def _():
             finish(i - 1)
 
-        @pl.when(i == keep)
-        def _():
-            lead_sent(1)
-
-        @pl.when(i > keep)
+        @pl.when(i >= keep)
         def _():
             swap(i - keep, 1).wait_send()
 
         product(i, 1, wu)
+
+        @pl.when(i > 3)
+        def _():
+            stage(i - 3)
+
+        retire(i - 1)
 
         @pl.when(i < n - 1)
         def _():
@@ -345,12 +340,6 @@
             scale_ring(i).wait_recv()
             scale_on(i + 1)
 
-        retire(i - 1)
-
-        @pl.when(i > 3)
-        def _():
-            stage(i - 3)
-
         @pl.when(i == n - 1)
         def _():
             finish(i - 1)
@@ -369,12 +358,12 @@
 
             down(i - 2)
 
+    stage(n - 3)
     retire(n - 1)
-    stage(n - 3)
-    share(1).wait_send()
-    share(2).wait_send()
     rv[0, col] = kept[...]
     finish(n - 1)
+    again = (n - 1) // keep * keep
+    share(again).wait_send()
     share(0).start()
     sent(n - 4)
     ring_free(n - 2)
@@ -402,17 +391,11 @@
         swap(s, 0).wait_send()
         swap(s, 1).wait_send()
 
-    @pl.loop(0, n)
-    def _(s):
-        @pl.when((s < 1) | (s > 2))
-        def _():
-            share(s).wait_send()
-
-        scale_sib(s).wait_send()
-
-        @pl.when(s < n - 1)
-        def _():
-            scale_ring(s).wait_send()
+    for s in [0] + [s for s in range(n - keep, n) if s != again]:
+        share(s).wait_send()
+    scale_sib(n - 2).wait_send()
+    scale_ring(n - 2).wait_send()
+    scale_sib(n - 1).wait_send()
 
 
 def kernels(rows, cols, tokens, norm_gain, gate_proj, up_proj, down_proj):
@@ -443,12 +426,10 @@
             pltpu.VMEM((2, half, 128), F32),
             pltpu.VMEM((half, 128), F32),
             pltpu.VMEM((n, 2, half, 128), F32),
-            dma, dma((units // lead,)), dma((units // lead,)), dma, dma((2,)),
-            dma((n, 2)), dma((n, 2)), dma((n, 2)), dma((n, 2)),
-            dma((2, units // lead)), dma((2, units // lead)),
-            dma((n, 3)), dma((n, 3)),
-            dma((n, parts)), dma((n, parts)), dma((n, 2, parts)), dma((n, 2, parts)),
-            dma((n, 2)), dma((n, 2)),
+            dma, dma((units // lead,)), dma, dma((2,)),
+            dma((2, 2)), dma((n, 2)), dma((2,)), dma((n,)), dma((4, 3)), dma((4, 3)),
+            dma((2, parts)), dma((3, parts)), dma((2, 2, parts)), dma((3, 2, parts)),
+            dma((2, 2)), dma((n, 2)),
             pltpu.SemaphoreType.REGULAR((n, 3)),
         ],
         compiler_params=pltpu.CompilerParams(

time: 140 us -> 137 us (0.979)
  Pallas kernels: 138 us -> 135 us
    pallas_call x1, Pallas kernels: 138 us -> 135 us  [kernels(): pl.pallas_call(functools.partial(fused_kernel, rows, cols, tile, lead), o...]
where the time goes in v2:
time: 137 us
  Pallas kernels  135 us (99%)
  local copies, waits for them, and re-layouts  1.87 us (1%)
    pallas_call x1, Pallas kernels, kernels(): pl.pallas_call(functools.partial(fused_kernel, rows, cols, tile, lead), o...  135 us

profile of v2, /device:TPU:0, one launch (start us, length us, event | category | flops | bytes accessed | tf_op | source)
XLA Modules:
  0.0 136.7 jit_solution(1486795327468256772)
XLA Ops:
  0.0 134.9 %shard_map.55 = bf16[64,4096]{1,0:T(8,128)(2,1)} custom-call(bf16[64,4096]{1,0:T(8,128)(2,1)} %tok_hbm.1, bf16[32,128]{1,0:T(8,128)(2,1)} %bitcast.1, bf16[4096,1792]{1,0:T(8,128)(2,1)} %wg_hbm.1, bf16[4096,1792]{1,0:T(8,128)(2,1)} %wu_hbm.1, bf16[1792,4096]{1,0:T(8,128)(2,1)} %wd_hbm.1), custom_call_target="tpu_custom_call" | custom-call | tf_op jit(solution)/shard_map/pallas_call | solution.py:412
  134.9 1.9 %copy.7 = bf16[64,4096]{1,0:T(8,128)(2,1)} copy(bf16[64,4096]{1,0:T(8,128)(2,1)} %shard_map.55) | data formatting | bytes 1048576

commit v3 on v2

--- a/solution.py
+++ b/solution.py
@@ -266,11 +266,28 @@
     pass_on(0)
     trade = remote(sq.at[1 - col], sq_in, sq_sem.at[0], sq_sem.at[1], across)
     trade.start()
-    with jax.named_scope("sib0"):
-        sib(0).wait_recv()
+    early = min(3, leads - 2)
+
+    def lead_rows(t, c):
+        at, rows_at = lead_cols(t), pl.ds(pl.multiple_of(c * half, half), half)
+        part = jnp.dot(x[0, :, c].reshape(2 * half, width), wg[:, at], preferred_element_type=F32)
+        pb[0, 0, :, rows_at, at] = part.astype(BF).reshape(2, half, lead)
+        remote(pb.at[0, 0, 1 - col, rows_at, at], rv.at[0, 0, rows_at, at], y_s.at[0, 0], y_r.at[0, 0], across).start()
+
+    @pl.loop(0, early)
+    def _(t):
+        load_g(t).wait()
+        lead_rows(t, core)
+
+    sib(0).wait_recv()
+
+    @pl.loop(0, early)
+    def _(t):
+        lead_rows(t, 1 - core)
+        load_u(t).start()
 
     def lead_product(g, w, load):
-        @pl.loop(0, leads)
+        @pl.loop(0 if g else early, leads)
         def _(t):
             load(t).wait()
             at = lead_cols(t)

time: 137 us -> 137 us (level)
  no operation moved by 1% of the time
where the time goes in v3:
time: 137 us; the launch traced here: 136 us
  Pallas kernels  135 us (99%)
  local copies, waits for them, and re-layouts  1.87 us (1%)
    pallas_call x1, Pallas kernels, kernels(): pl.pallas_call(functools.partial(fused_kernel, rows, cols, tile, lead), o...  135 us

profile of v3, /device:TPU:0, one launch (start us, length us, event | category | flops | bytes accessed | tf_op | source)
XLA Modules:
  0.0 136.4 jit_solution(1884647701695155867)
XLA Ops:
  0.0 134.5 %shard_map.55 = bf16[64,4096]{1,0:T(8,128)(2,1)} custom-call(bf16[64,4096]{1,0:T(8,128)(2,1)} %tok_hbm.1, bf16[32,128]{1,0:T(8,128)(2,1)} %bitcast.1, bf16[4096,1792]{1,0:T(8,128)(2,1)} %wg_hbm.1, bf16[4096,1792]{1,0:T(8,128)(2,1)} %wu_hbm.1, bf16[1792,4096]{1,0:T(8,128)(2,1)} %wd_hbm.1), custom_call_target="tpu_custom_call" | custom-call | tf_op jit(solution)/shard_map/pallas_call | solution.py:429
  134.6 1.9 %copy.7 = bf16[64,4096]{1,0:T(8,128)(2,1)} copy(bf16[64,4096]{1,0:T(8,128)(2,1)} %shard_map.55) | data formatting | bytes 1048576
